TPU v7x, 512 devices: a whole 4x8x8 slice. The times are simulated.
512 devices in a mesh: slab: 64 (over z, x, core), tile: 8 (over y).
Axes of the slice: x: 4, y: 8, z: 8, core: 2. Of those that a mesh axis runs over, the one named last changes fastest.
Arguments:
- features: bfloat16 [64, 8, 512, 128], P('slab', 'tile'), may hold values from -24 to 24
- counts: int32 [64, 8], P('slab', 'tile'), may hold values from 128 to 512, as said below
- rulebook: int32 [64, 8, 27, 512], P('slab', 'tile'), may hold values from 0 to 800, as said below
- face_rows: int32 [64, 8, 4, 64], P('slab', 'tile'), may hold values from 0 to 511, as said below
- conv_one: bfloat16 [27, 128, 128], replicated, may hold values from -0.109375 to 0.109375
- gain_one: float32 [128], replicated, may hold values from 0.5 to 1.5
- shift_one: float32 [128], replicated, may hold values from -0.5 to 0.5
- conv_two: bfloat16 [27, 128, 128], replicated, may hold values from -0.109375 to 0.109375
- gain_two: float32 [128], replicated, may hold values from 0.5 to 1.5
- shift_two: float32 [128], replicated, may hold values from -0.5 to 0.5
Outputs:
- output: bfloat16 [64, 8, 512, 128], P('slab', 'tile')
Inputs may be any that keep to these rules, and one draw needn't show every extreme that they name: `counts`: each device's voxels fill its 8 x 8 grid columns with the same number each, between 2 and 8; some device of the highest slab index holds 512. `rulebook`: an entry names the extended-table row that holds the voxel's neighbour at offset k = 9 (dx + 1) + 3 (dy + 1) + (dz + 1) of the submanifold 3x3x3 stencil, or 800 where that cell is inactive or outside the grid; the voxel itself is at offset 13; rows at or past the device's count name 800 at every offset. `face_rows`: lists 0 to 3 hold the device's voxels on its lower and higher face along the first, then the lower and higher face along the second dimension; the j-th voxel of the i-th column along a face stands at position i * 8 + j; unused positions name row 0.
All inputs are finite; a program needn't handle non-finite values.
Results may differ from a plain program's by a relative error of at most 0.0033.
Values may be sent and summed in bfloat16 or wider, within the bound.
A program may use at most 64 MiB of HBM per device.

v0:
```python
from functools import partial

import jax
import jax.numpy as jnp
from jax import lax
from jax.sharding import Mesh
from jax.sharding import PartitionSpec as P

SIDE = 8
SLAB = ("slab_0", "slab_1", "slab_2")
SLAB_TILE = ("slab_0", "slab_1", "slab_2", "tile")


EPSILON = 1e-05


def extended(block, sides, width):
    for axis, dim in sides:
        count = lax.axis_size(axis)
        forward = [(i, i + 1) for i in range(count - 1)]
        backward = [(target, source) for source, target in forward]
        low = lax.ppermute(
            lax.slice_in_dim(block, block.shape[dim] - width, None, axis=dim), axis, forward
        )
        high = lax.ppermute(lax.slice_in_dim(block, 0, width, axis=dim), axis, backward)
        block = jnp.concatenate([low, block, high], axis=dim)
    return block


def by_axis(shard, axes):
    for axis in axes:
        shard = lax.psum(shard, axis)
    return shard


def build_table(local_rows, face_lists):
    face_len = face_lists.shape[1]
    column = face_len // SIDE
    picked = local_rows[face_lists]
    tile_recv = extended(picked[2:4], (("tile", 0),), 1)
    core_low = tile_recv[0]
    core_high = tile_recv[3]
    slab_send = jnp.stack(
        [
            jnp.concatenate([picked[0], core_low[:column], core_high[:column]], axis=0),
            jnp.concatenate(
                [picked[1], core_low[face_len - column :], core_high[face_len - column :]], axis=0
            ),
        ]
    )
    slab_recv = extended(slab_send, ((SLAB, 0),), 1)
    low_full = slab_recv[0]
    high_full = slab_recv[3]
    slab_low = low_full[:face_len]
    slab_high = high_full[:face_len]
    tile_low = jnp.concatenate(
        [low_full[face_len : face_len + column], core_low, high_full[face_len : face_len + column]],
        axis=0,
    )
    tile_high = jnp.concatenate(
        [low_full[face_len + column :], core_high, high_full[face_len + column :]], axis=0
    )
    zero_row = jnp.zeros((1, local_rows.shape[1]), local_rows.dtype)
    return jnp.concatenate([local_rows, slab_low, slab_high, tile_low, tile_high, zero_row], axis=0)


def pick_rows(lookup, tap_index, offset, block_rows, flat_weight):
    gathered = jnp.take(lookup, tap_index.T, axis=0)
    gathered = gathered.reshape(block_rows, tap_index.shape[0] * lookup.shape[1])
    return jnp.dot(gathered, flat_weight, preferred_element_type=jnp.float32)


def convolve(lookup, tap_index, weight):
    total_rows = tap_index.shape[1]
    block_rows = min(512, total_rows)
    flat_weight = weight.reshape(weight.shape[0] * weight.shape[1], weight.shape[2])
    compute = partial(pick_rows, lookup, tap_index, 0, block_rows, flat_weight)
    result = compute()
    return result


def normalize(conv_out, live_mask, count_value, gain, shift):
    first_sum = jnp.sum(conv_out * live_mask, axis=0)
    square_sum = jnp.sum(conv_out * conv_out * live_mask, axis=0)
    channel_sums, square_sums, voxel_total = (
        by_axis(first_sum, SLAB_TILE),
        by_axis(square_sum, SLAB_TILE),
        by_axis(count_value, SLAB_TILE),
    )
    average = channel_sums / voxel_total
    variance = square_sums / voxel_total - average * average
    return (conv_out - average) * lax.rsqrt(variance + EPSILON) * gain + shift


def per_device(
    features,
    counts,
    rulebook,
    face_rows,
    conv_one,
    gain_one,
    shift_one,
    conv_two,
    gain_two,
    shift_two,
):
    local_rows = features[0, 0]
    face_lists = face_rows[0, 0]
    tap_index = rulebook[0, 0]
    voxel_count = counts[0, 0]
    count_value = voxel_count.astype(jnp.float32)
    live_mask = (lax.broadcasted_iota(jnp.int32, (local_rows.shape[0], 1), 0) < voxel_count).astype(
        jnp.float32
    )
    first = convolve(build_table(local_rows, face_lists), tap_index, conv_one)
    hidden = (
        live_mask * jnp.maximum(normalize(first, live_mask, count_value, gain_one, shift_one), 0.0)
    ).astype(jnp.bfloat16)
    second = convolve(build_table(hidden, face_lists), tap_index, conv_two)
    summed = normalize(second, live_mask, count_value, gain_two, shift_two) + local_rows.astype(
        jnp.float32
    )
    output = (live_mask * jnp.maximum(summed, 0.0)).astype(jnp.bfloat16)
    return output[None, None]


def solution(mesh):
    torus = Mesh(
        mesh.devices.reshape(8, 4, 2, mesh.shape["tile"]), ("slab_0", "slab_1", "slab_2", "tile")
    )
    in_specs = (
        P(SLAB, "tile", None, None),
        P(SLAB, "tile"),
        P(SLAB, "tile", None, None),
        P(SLAB, "tile", None, None),
        P(),
        P(),
        P(),
        P(),
        P(),
        P(),
    )
    out_specs = P(SLAB, "tile", None, None)
    return jax.shard_map(
        per_device, mesh=torus, in_specs=in_specs, out_specs=out_specs, check_vma=False
    )
```

profile of v0, /device:TPU:1, one launch (start us, length us, event | category | flops | bytes accessed | tf_op | source)
XLA Modules:
  0.0 228.1 jit_solution(8170010614980495106)
XLA Ops:
  0.0 0.0 copy-start
  0.0 0.8 compare_select_fusion.1
  0.8 0.1 reshape.90
  0.9 1.6 gather_fusion
  2.5 4.0 %collective-permute-start = (bf16[1,64,128]{2,1,0:T(8,128)(2,1)S(1)}, bf16[1,64,128]{2,1,0:T(8,128)(2,1)S(1)}, u32[]{:S(2)}, u32[]{:S(2)}) collective-permute-start(bf16[1,64,128]{2,1,0:T(8,128)(2,1)S(1)} %get-tuple-element.42), channel_id=1, source_target_pairs={{0,1},{1,2},{2,3},{3,4},{4,5},{5,6},{6,7},{8,9},{9,10},{10,11},{11... | collective-permute-start | bytes 49160 | tf_op jit(solution)/shard_map/ppermute | solution.py:22
  6.5 1.3 collective-permute-start.1
  7.8 0.9 constant_dynamic-update-slice_fusion.9
  8.8 0.8 compare_select_fusion
  9.6 0.8 compare_and_fusion
  10.4 0.1 copy.15
  10.6 0.2 reshape.122
  11.5 0.2 copy.13
  11.7 0.0 collective-permute-done
  11.7 0.0 collective-permute-done.1
  11.7 4.4 %collective-permute-start.2 = (bf16[1,80,128]{2,1,0:T(8,128)(2,1)S(1)}, bf16[1,80,128]{2,1,0:T(8,128)(2,1)S(1)}, u32[]{:S(2)}, u32[]{:S(2)}) collective-permute-start(bf16[1,80,128]{2,1,0:T(8,128)(2,1)S(1)} %maximum_bitcast_fusion), channel_id=1, source_target_pairs={{0,8},{8,16},{16,24},{24,32},{32,40},{40,48},{48,56},{56,64},{64,7... | collective-permute-start | bytes 61448 | tf_op jit(solution)/shard_map/ppermute | solution.py:22
  16.2 3.3 %collective-permute-start.3 = (bf16[1,80,128]{2,1,0:T(8,128)(2,1)S(1)}, bf16[1,80,128]{2,1,0:T(8,128)(2,1)S(1)}, u32[]{:S(2)}, u32[]{:S(2)}) collective-permute-start(bf16[1,80,128]{2,1,0:T(8,128)(2,1)S(1)} %maximum_bitcast_fusion.1), channel_id=1, source_target_pairs={{8,0},{16,8},{24,16},{32,24},{40,32},{48,40},{56,48},{64,56},{72,6... | collective-permute-start | bytes 61448 | tf_op jit(solution)/shard_map/ppermute | solution.py:25
  19.5 0.0 collective-permute-done.2
  19.5 1.7 collective-permute-done.3
  21.3 28.4 %gather_fusion.2 = bf16[13824,128]{1,0:T(8,128)(2,1)} fusion(bf16[801,128]{1,0:T(8,128)(2,1)S(1)} %constant_dynamic-update-slice_fusion, s32[14336]{0:T(1024)S(1)} %pad_clamp_fusion), kind=kCustom, calls=%fused_computation.clone | custom fusion | bytes 7133184 | tf_op jit(solution)/shard_map/jit(_take)/gather | solution.py:68
  49.7 6.6 %reshape.125 = bf16[512,27,128]{2,1,0:T(8,128)(2,1)} reshape(bf16[13824,128]{1,0:T(8,128)(2,1)} %gather_fusion.2) | data formatting | bytes 7077888 | tf_op jit(solution)/shard_map/jit(_take)/gather | solution.py:68
  56.3 10.1 %broadcast_select_fusion = bf16[512,27,128]{2,1,0:T(8,128)(2,1)S(1)} fusion(bf16[512,27,128]{2,1,0:T(8,128)(2,1)} %reshape.125, pred[512,27]{1,0:T(8,128)(4,1)S(1)} %copy.13), kind=kLoop, calls=%fused_computation.4 | loop fusion | flops 1769472 | bytes 7091712 | tf_op jit(solution)/shard_map/jit(_take)/select_n | solution.py:68
  66.4 0.0 copy-done
  66.4 0.0 copy-start.2
  66.4 0.0 copy-start.3
  66.4 1.3 multiply_reduce_fusion.2
  67.7 20.1 %all-reduce.3 = (f32[128]{0:T(128)S(1)}, f32[]{:T(128)}, f32[128]{0:T(128)S(1)}) all-reduce(f32[128]{0:T(128)S(1)} %get-tuple-element.9, f32[]{:T(128)S(6)} %convert_element_type.21, f32[128]{0:T(128)S(1)} %get-tuple-element.8), channel_id=1, replica_groups=mesh['slab_0'=8,'slab_1'=4,'slab_2'=2,'tile'=8] {'slab_0'}, use_global_device_ids=true, to_apply=%region_1.3 | all-reduce | flops 257 | bytes 2056 | tf_op jit(solution)/shard_map/psum | solution.py:32
  87.8 9.4 %all-reduce.5 = (f32[128]{0:T(128)S(1)}, f32[]{:T(128)}, f32[128]{0:T(128)S(1)}) all-reduce(f32[128]{0:T(128)S(1)} %get-tuple-element.17, f32[]{:T(128)} %get-tuple-element.18, f32[128]{0:T(128)S(1)} %get-tuple-element.19), channel_id=1, replica_groups=mesh['slab_0'=8,'slab_1'=4,'slab_2'=2,'tile'=8] {'slab_1'}, use_global_device_ids=true, to_apply=%region_2.4 | all-reduce | flops 257 | bytes 2056 | tf_op jit(solution)/shard_map/psum | solution.py:32
  97.2 7.0 %all-reduce.7 = (f32[128]{0:T(128)S(1)}, f32[]{:T(128)}, f32[128]{0:T(128)S(1)}) all-reduce(f32[128]{0:T(128)S(1)} %get-tuple-element.22, f32[]{:T(128)} %get-tuple-element.23, f32[128]{0:T(128)S(1)} %get-tuple-element.24), channel_id=1, replica_groups=mesh['slab_0'=8,'slab_1'=4,'slab_2'=2,'tile'=8] {'slab_2'}, use_global_device_ids=true, to_apply=%region_3.5 | all-reduce | flops 257 | bytes 2056 | tf_op jit(solution)/shard_map/psum | solution.py:32
  104.2 15.1 %all-reduce.1 = (f32[128]{0:T(128)S(1)}, f32[]{:T(128)}, f32[128]{0:T(128)S(1)}) all-reduce(f32[128]{0:T(128)S(1)} %get-tuple-element.27, f32[]{:T(128)} %get-tuple-element.28, f32[128]{0:T(128)S(1)} %get-tuple-element.29), channel_id=1, replica_groups=mesh['slab_0'=8,'slab_1'=4,'slab_2'=2,'tile'=8] {'tile'}, use_global_device_ids=true, to_apply=%region_4.6 | all-reduce | flops 257 | bytes 2056 | tf_op jit(solution)/shard_map/psum | solution.py:32
  119.3 0.7 add_rsqrt_fusion.1
  120.0 0.0 copy-done.2
  120.0 0.0 copy-done.3
  120.0 0.1 constant_dynamic-update-slice_fusion.19
  120.1 0.9 gather_fusion.1
  121.0 2.5 %collective-permute-start.4 = (bf16[1,64,128]{2,1,0:T(8,128)(2,1)S(1)}, bf16[1,64,128]{2,1,0:T(8,128)(2,1)S(1)}, u32[]{:S(2)}, u32[]{:S(2)}) collective-permute-start(bf16[1,64,128]{2,1,0:T(8,128)(2,1)S(1)} %get-tuple-element.38), channel_id=1, source_target_pairs={{0,1},{1,2},{2,3},{3,4},{4,5},{5,6},{6,7},{8,9},{9,10},{10,11},{11... | collective-permute-start | bytes 49160 | tf_op jit(solution)/shard_map/ppermute | solution.py:22
  123.5 1.3 collective-permute-start.5
  124.8 0.0 collective-permute-done.4
  124.8 3.2 %collective-permute-done.5 = bf16[1,64,128]{2,1,0:T(8,128)(2,1)S(1)} collective-permute-done((bf16[1,64,128]{2,1,0:T(8,128)(2,1)S(1)}, bf16[1,64,128]{2,1,0:T(8,128)(2,1)S(1)}, u32[]{:S(2)}, u32[]{:S(2)}) %collective-permute-start.5) | collective-permute-done | bytes 16416 | tf_op jit(solution)/shard_map/ppermute | solution.py:25
  128.0 8.3 %collective-permute-start.6 = (bf16[1,80,128]{2,1,0:T(8,128)(2,1)S(1)}, bf16[1,80,128]{2,1,0:T(8,128)(2,1)S(1)}, u32[]{:S(2)}, u32[]{:S(2)}) collective-permute-start(bf16[1,80,128]{2,1,0:T(8,128)(2,1)S(1)} %maximum_bitcast_fusion.2), channel_id=1, source_target_pairs={{0,8},{8,16},{16,24},{24,32},{32,40},{40,48},{48,56},{56,64},{64,7... | collective-permute-start | bytes 61448 | tf_op jit(solution)/shard_map/ppermute | solution.py:22
  136.3 1.9 collective-permute-start.7
  138.2 0.0 collective-permute-done.6
  138.3 3.1 %collective-permute-done.7 = bf16[1,80,128]{2,1,0:T(8,128)(2,1)S(1)} collective-permute-done((bf16[1,80,128]{2,1,0:T(8,128)(2,1)S(1)}, bf16[1,80,128]{2,1,0:T(8,128)(2,1)S(1)}, u32[]{:S(2)}, u32[]{:S(2)}) %collective-permute-start.7) | collective-permute-done | bytes 20512 | tf_op jit(solution)/shard_map/ppermute | solution.py:25
  141.5 28.4 %gather_fusion.3 = bf16[13824,128]{1,0:T(8,128)(2,1)} fusion(bf16[801,128]{1,0:T(8,128)(2,1)S(1)} %constant_dynamic-update-slice_fusion.10, s32[14336]{0:T(1024)S(1)} %pad_clamp_fusion), kind=kCustom, calls=%fused_computation.1.clone | custom fusion | bytes 7133184 | tf_op jit(solution)/shard_map/jit(_take)/gather | solution.py:68
  169.9 6.6 %reshape.129 = bf16[512,27,128]{2,1,0:T(8,128)(2,1)} reshape(bf16[13824,128]{1,0:T(8,128)(2,1)} %gather_fusion.3) | data formatting | bytes 7077888 | tf_op jit(solution)/shard_map/jit(_take)/gather | solution.py:68
  176.5 0.0 copy-start.6
  176.5 10.1 %broadcast_select_fusion.1 = bf16[512,27,128]{2,1,0:T(8,128)(2,1)S(1)} fusion(bf16[512,27,128]{2,1,0:T(8,128)(2,1)} %reshape.129, pred[512,27]{1,0:T(8,128)(4,1)S(1)} %copy.13), kind=kLoop, calls=%fused_computation.5 | loop fusion | flops 1769472 | bytes 7091712 | tf_op jit(solution)/shard_map/jit(_take)/select_n | solution.py:68
  186.6 0.0 copy-done.6
  186.6 0.0 copy-start.1
  186.6 0.0 copy-start.4
  186.7 0.0 copy-start.5
  186.7 1.2 multiply_reduce_fusion
  187.9 10.7 %all-reduce.2 = (f32[128]{0:T(128)S(1)}, f32[128]{0:T(128)S(1)}) all-reduce(f32[128]{0:T(128)S(1)} %get-tuple-element.7, f32[128]{0:T(128)S(1)} %get-tuple-element.6), channel_id=1, replica_groups=mesh['slab_0'=8,'slab_1'=4,'slab_2'=2,'tile'=8] {'slab_0'}, use_global_device_ids=true, to_apply=%region_15.17 | all-reduce | flops 256 | bytes 2048 | tf_op jit(solution)/shard_map/psum | solution.py:32
  198.6 10.2 %all-reduce.4 = (f32[128]{0:T(128)S(1)}, f32[128]{0:T(128)S(1)}) all-reduce(f32[128]{0:T(128)S(1)} %get-tuple-element.15, f32[128]{0:T(128)S(1)} %get-tuple-element.16), channel_id=1, replica_groups=mesh['slab_0'=8,'slab_1'=4,'slab_2'=2,'tile'=8] {'slab_1'}, use_global_device_ids=true, to_apply=%region_16.18 | all-reduce | flops 256 | bytes 2048 | tf_op jit(solution)/shard_map/psum | solution.py:32
  208.8 4.0 %all-reduce.6 = (f32[128]{0:T(128)S(1)}, f32[128]{0:T(128)S(1)}) all-reduce(f32[128]{0:T(128)S(1)} %get-tuple-element.20, f32[128]{0:T(128)S(1)} %get-tuple-element.21), channel_id=1, replica_groups=mesh['slab_0'=8,'slab_1'=4,'slab_2'=2,'tile'=8] {'slab_2'}, use_global_device_ids=true, to_apply=%region_17.19 | all-reduce | flops 256 | bytes 2048 | tf_op jit(solution)/shard_map/psum | solution.py:32
  212.8 13.8 %all-reduce = (f32[128]{0:T(128)S(1)}, f32[128]{0:T(128)S(1)}) all-reduce(f32[128]{0:T(128)S(1)} %get-tuple-element.25, f32[128]{0:T(128)S(1)} %get-tuple-element.26), channel_id=1, replica_groups=mesh['slab_0'=8,'slab_1'=4,'slab_2'=2,'tile'=8] {'tile'}, use_global_device_ids=true, to_apply=%region_18.20 | all-reduce | flops 256 | bytes 2048 | tf_op jit(solution)/shard_map/psum | solution.py:32
  226.6 0.7 add_rsqrt_fusion
  227.3 0.0 copy-done.1
  227.3 0.0 copy-done.4
  227.3 0.0 copy-done.5
  227.3 0.8 fusion.10
  (31 shorter events, 0.2 us)
Async XLA Ops:
  0.0 66.4 %copy-start = (bf16[27,128,128]{2,1,0:T(8,128)(2,1)S(1)}, bf16[27,128,128]{2,1,0:T(8,128)(2,1)}, u32[]{:S(2)}) copy-start(bf16[27,128,128]{2,1,0:T(8,128)(2,1)} %param.16) | copy-start | bytes 2654212
  2.5 9.1 %collective-permute-start = (bf16[1,64,128]{2,1,0:T(8,128)(2,1)S(1)}, bf16[1,64,128]{2,1,0:T(8,128)(2,1)S(1)}, u32[]{:S(2)}, u32[]{:S(2)}) collective-permute-start(bf16[1,64,128]{2,1,0:T(8,128)(2,1)S(1)} %get-tuple-element.42), channel_id=1, source_target_pairs={{0,1},{1,2},{2,3},{3,4},{4,5},{5,6},{6,7},{8,9},{9,10},{10,11},{11... | collective-permute-start | bytes 49160 | tf_op jit(solution)/shard_map/ppermute | solution.py:22
  6.5 5.1 %collective-permute-start.1 = (bf16[1,64,128]{2,1,0:T(8,128)(2,1)S(1)}, bf16[1,64,128]{2,1,0:T(8,128)(2,1)S(1)}, u32[]{:S(2)}, u32[]{:S(2)}) collective-permute-start(bf16[1,64,128]{2,1,0:T(8,128)(2,1)S(1)} %get-tuple-element.41), channel_id=1, source_target_pairs={{1,0},{2,1},{3,2},{4,3},{5,4},{6,5},{7,6},{9,8},{10,9},{11,10},{12... | collective-permute-start | bytes 49160 | tf_op jit(solution)/shard_map/ppermute | solution.py:25
  11.7 7.8 %collective-permute-start.2 = (bf16[1,80,128]{2,1,0:T(8,128)(2,1)S(1)}, bf16[1,80,128]{2,1,0:T(8,128)(2,1)S(1)}, u32[]{:S(2)}, u32[]{:S(2)}) collective-permute-start(bf16[1,80,128]{2,1,0:T(8,128)(2,1)S(1)} %maximum_bitcast_fusion), channel_id=1, source_target_pairs={{0,8},{8,16},{16,24},{24,32},{32,40},{40,48},{48,56},{56,64},{64,7... | collective-permute-start | bytes 61448 | tf_op jit(solution)/shard_map/ppermute | solution.py:22
  16.2 5.1 %collective-permute-start.3 = (bf16[1,80,128]{2,1,0:T(8,128)(2,1)S(1)}, bf16[1,80,128]{2,1,0:T(8,128)(2,1)S(1)}, u32[]{:S(2)}, u32[]{:S(2)}) collective-permute-start(bf16[1,80,128]{2,1,0:T(8,128)(2,1)S(1)} %maximum_bitcast_fusion.1), channel_id=1, source_target_pairs={{8,0},{16,8},{24,16},{32,24},{40,32},{48,40},{56,48},{64,56},{72,6... | collective-permute-start | bytes 61448 | tf_op jit(solution)/shard_map/ppermute | solution.py:25
  66.4 53.6 %copy-start.2 = (f32[128]{0:T(128)S(1)}, f32[128]{0:T(128)}, u32[]{:S(2)}) copy-start(f32[128]{0:T(128)} %param.18) | copy-start | bytes 1540
  66.4 53.6 %copy-start.3 = (f32[128]{0:T(128)S(1)}, f32[128]{0:T(128)}, u32[]{:S(2)}) copy-start(f32[128]{0:T(128)} %param.17) | copy-start | bytes 1540
  121.0 3.8 %collective-permute-start.4 = (bf16[1,64,128]{2,1,0:T(8,128)(2,1)S(1)}, bf16[1,64,128]{2,1,0:T(8,128)(2,1)S(1)}, u32[]{:S(2)}, u32[]{:S(2)}) collective-permute-start(bf16[1,64,128]{2,1,0:T(8,128)(2,1)S(1)} %get-tuple-element.38), channel_id=1, source_target_pairs={{0,1},{1,2},{2,3},{3,4},{4,5},{5,6},{6,7},{8,9},{9,10},{10,11},{11... | collective-permute-start | bytes 49160 | tf_op jit(solution)/shard_map/ppermute | solution.py:22
  123.5 4.5 %collective-permute-start.5 = (bf16[1,64,128]{2,1,0:T(8,128)(2,1)S(1)}, bf16[1,64,128]{2,1,0:T(8,128)(2,1)S(1)}, u32[]{:S(2)}, u32[]{:S(2)}) collective-permute-start(bf16[1,64,128]{2,1,0:T(8,128)(2,1)S(1)} %get-tuple-element.37), channel_id=1, source_target_pairs={{1,0},{2,1},{3,2},{4,3},{5,4},{6,5},{7,6},{9,8},{10,9},{11,10},{12... | collective-permute-start | bytes 49160 | tf_op jit(solution)/shard_map/ppermute | solution.py:25
  128.0 10.3 %collective-permute-start.6 = (bf16[1,80,128]{2,1,0:T(8,128)(2,1)S(1)}, bf16[1,80,128]{2,1,0:T(8,128)(2,1)S(1)}, u32[]{:S(2)}, u32[]{:S(2)}) collective-permute-start(bf16[1,80,128]{2,1,0:T(8,128)(2,1)S(1)} %maximum_bitcast_fusion.2), channel_id=1, source_target_pairs={{0,8},{8,16},{16,24},{24,32},{32,40},{40,48},{48,56},{56,64},{64,7... | collective-permute-start | bytes 61448 | tf_op jit(solution)/shard_map/ppermute | solution.py:22
  136.3 5.1 %collective-permute-start.7 = (bf16[1,80,128]{2,1,0:T(8,128)(2,1)S(1)}, bf16[1,80,128]{2,1,0:T(8,128)(2,1)S(1)}, u32[]{:S(2)}, u32[]{:S(2)}) collective-permute-start(bf16[1,80,128]{2,1,0:T(8,128)(2,1)S(1)} %maximum_bitcast_fusion.3), channel_id=1, source_target_pairs={{8,0},{16,8},{24,16},{32,24},{40,32},{48,40},{56,48},{64,56},{72,6... | collective-permute-start | bytes 61448 | tf_op jit(solution)/shard_map/ppermute | solution.py:25
  176.5 10.2 %copy-start.6 = (bf16[27,128,128]{2,1,0:T(8,128)(2,1)S(1)}, bf16[27,128,128]{2,1,0:T(8,128)(2,1)}, u32[]{:S(2)}) copy-start(bf16[27,128,128]{2,1,0:T(8,128)(2,1)} %param.19) | copy-start | bytes 2654212
  186.6 40.7 %copy-start.1 = (bf16[1,1,512,128]{3,2,1,0:T(8,128)(2,1)S(1)}, bf16[1,1,512,128]{3,2,1,0:T(8,128)(2,1)}, u32[]{:S(2)}) copy-start(bf16[1,1,512,128]{3,2,1,0:T(8,128)(2,1)} %param.12) | copy-start | bytes 393220
  186.6 40.7 %copy-start.4 = (f32[128]{0:T(128)S(1)}, f32[128]{0:T(128)}, u32[]{:S(2)}) copy-start(f32[128]{0:T(128)} %param.21) | copy-start | bytes 1540
  186.7 40.7 %copy-start.5 = (f32[128]{0:T(128)S(1)}, f32[128]{0:T(128)}, u32[]{:S(2)}) copy-start(f32[128]{0:T(128)} %param.20) | copy-start | bytes 1540
where the time goes:
time: 233 us; the launch traced here: 228 us
  blocking collectives  90.3 us (39%)
  local copies, waits for them, and re-layouts  74.2 us (32%)
  starting transfers between devices  27.1 us (12%)
  other arithmetic  24.9 us (11%)
  waiting for transfers between devices  8.04 us (3%)
  matrix products  2.55 us (1%)
    psum x8, blocking collectives, by_axis(): shard = lax.psum(shard, axis)  90.3 us
    gather x4, local copies, waits for them, and re-layouts, pick_rows(): gathered = jnp.take(lookup, tap_index.T, axis=0)  69.9 us
    select_n x3, other arithmetic, pick_rows(): gathered = jnp.take(lookup, tap_index.T, axis=0)  21 us
    ppermute x4, starting transfers between devices, extended(): lax.ppermute(lax.slice_in_dim(block, block.shape[dim] - width, None, axis...  19.2 us
    ppermute x4, waiting for transfers between devices, extended(): lax.ppermute(lax.slice_in_dim(block, 0, width, axis=dim), axis, backward)  8.03 us
    ppermute x4, starting transfers between devices, extended(): lax.ppermute(lax.slice_in_dim(block, 0, width, axis=dim), axis, backward)  7.85 us
  transfers between devices with their start and end apart: 8, of which 3 were waited for; matrix products, arithmetic and copies ran while one was open for 1% of the time, Pallas kernels for 0%

commit v1 on v0

v1 whole, which is shorter than its diff:
```python
import functools

import jax
import jax.numpy as jnp
from jax import lax
from jax.experimental import pallas as pl
from jax.experimental.pallas import tpu as pltpu
from jax.sharding import PartitionSpec as P

MESH = pl.DeviceIdType.MESH
F32 = jnp.float32
BF16 = jnp.bfloat16
EPSILON = 1e-05
DEAD = -1e30
RING = 8
TAPS = 27
HALF = 256
HALO = 288


def thirds(x):
    high = x.astype(BF16)
    rest = x - high.astype(F32)
    middle = rest.astype(BF16)
    low = (rest - middle.astype(F32)).astype(BF16)
    return high, middle, low


def kernel(
    n_slab,
    n_tile,
    feat,
    counts,
    rb,
    face,
    w_one,
    gain_one,
    shift_one,
    w_two,
    gain_two,
    shift_two,
    out,
    weights,
    wt,
    face_hot,
    table,
    gathered,
    conv_out,
    send_face,
    halo,
    inbox,
    w_sem,
    halo_send,
    halo_recv,
    red_send,
    red_recv,
):
    s = lax.axis_index("slab")
    t = lax.axis_index("tile")
    rows = feat.shape[2]
    chans = feat.shape[3]
    up_s, down_s = lax.rem(s + 1, n_slab), lax.rem(s + n_slab - 1, n_slab)
    up_t, down_t = lax.rem(t + 1, n_tile), lax.rem(t + n_tile - 1, n_tile)
    sides = (
        (down_s, t),
        (up_s, t),
        (s, down_t),
        (s, up_t),
        (up_s, down_t),
        (up_s, up_t),
        (down_s, down_t),
        (down_s, up_t),
    )
    inner = lax.rem(s, RING)
    outer = s // RING

    def peer(phase, step):
        if phase == 0:
            return (s, lax.rem(t + step, RING))
        if phase == 1:
            return (outer * RING + lax.rem(inner + step, RING), t)
        return (lax.rem(outer + step, RING) * RING + inner, t)

    slot_of = (t, inner, outer)

    barrier = pltpu.get_barrier_semaphore()
    for device in sides:
        pl.semaphore_signal(barrier, inc=1, device_id=device, device_id_type=MESH)
    for phase in range(3):
        for step in range(1, RING):
            pl.semaphore_signal(
                barrier, inc=1, device_id=peer(phase, step), device_id_type=MESH
            )

    loads = [
        pltpu.make_async_copy(w, weights.at[i], w_sem.at[i])
        for i, w in enumerate((w_one, w_two))
    ]
    for load in loads:
        load.start()

    count = counts[0, 0]
    live = lax.broadcasted_iota(jnp.int32, (rows, chans), 0) < count
    features = feat[0, 0].astype(F32)

    row_id = lax.broadcasted_iota(jnp.int32, (rows, 64), 0)
    for j in range(4):
        hot = row_id == face[0, 0, j : j + 1, :]
        face_hot[:, j * 64 : (j + 1) * 64] = jnp.where(hot, 1.0, 0.0).astype(BF16)

    def start_exchange(e, source):
        parts = [p.astype(F32).T.astype(BF16) for p in thirds(source)]
        picked = jnp.dot(
            jnp.concatenate(parts, axis=0), face_hot[...], preferred_element_type=F32
        )
        total = picked[:chans] + picked[chans : 2 * chans] + picked[2 * chans :]
        send_face[e] = total.T
        moves = (
            (0, 64, 64),
            (64, 64, 0),
            (128, 64, 216),
            (192, 64, 136),
            (64, 8, 208),
            (120, 8, 128),
            (0, 8, 280),
            (56, 8, 200),
        )
        copies = []
        for i, (start, size, target) in enumerate(moves):
            copies.append(
                pltpu.make_async_remote_copy(
                    src_ref=send_face.at[e, pl.ds(start, size)],
                    dst_ref=halo.at[e, pl.ds(target, size)],
                    send_sem=halo_send.at[e, i],
                    recv_sem=halo_recv.at[e, i],
                    device_id=sides[i],
                    device_id_type=MESH,
                )
            )
        return copies

    has_down_s, has_up_s = s > 0, s < n_slab - 1
    has_down_t, has_up_t = t > 0, t < n_tile - 1

    def received(e, blank):
        pieces = (
            (0, 64, has_down_s),
            (64, 64, has_up_s),
            (128, 8, has_down_s & has_down_t),
            (136, 64, has_down_t),
            (200, 8, has_up_s & has_down_t),
            (208, 8, has_down_s & has_up_t),
            (216, 64, has_up_t),
            (280, 8, has_up_s & has_up_t),
        )
        return jnp.concatenate(
            [
                jnp.where(present, halo[e, pl.ds(start, size), :], blank)
                for start, size, present in pieces
            ],
            axis=0,
        )

    def convolve(c, local, around):
        pad = jnp.zeros((HALF + 64 - HALO, chans), F32)
        low = jnp.concatenate([around[:64], around[128:], pad], axis=0)
        high = jnp.concatenate([around[64:], pad], axis=0)
        for i in range(2):
            table[i, :chans] = local[:HALF].T.astype(BF16)
            table[i, chans : 2 * chans] = local[HALF:].T.astype(BF16)
        table[0, 2 * chans :] = low.T.astype(BF16)
        table[1, 2 * chans :] = high.T.astype(BF16)

        position = lax.broadcasted_iota(jnp.int32, (HALF, rows), 0)

        def tap(k, carry):
            index = rb[0, 0, pl.ds(k, 1), :]
            slot = jnp.where(
                index < 2 * HALF,
                index & (HALF - 1),
                jnp.where(index < 576, index - 512, index - 576),
            )
            hot = jnp.where(position == slot, 1.0, 0.0).astype(BF16)
            side = jnp.where(k < 9, 0, 1)
            found = jnp.dot(table[side], hot, preferred_element_type=F32)
            value = jnp.where(
                index < HALF,
                found[:chans],
                jnp.where(index < 2 * HALF, found[chans : 2 * chans], found[2 * chans :]),
            )
            gathered[pl.ds(pl.multiple_of(k * chans, chans), chans), :] = value.astype(BF16)
            return carry

        lax.fori_loop(0, TAPS, tap, 0)
        result = jnp.dot(wt[c], gathered[...], preferred_element_type=F32)
        conv_out[c] = result.T

    def transpose_weights(c):
        def one(k, carry):
            wt[c, :, pl.ds(pl.multiple_of(k * chans, chans), chans)] = weights[c, k].T
            return carry

        lax.fori_loop(0, TAPS, one, 0)

    copies = []

    def reduce_start(c, phase, value):
        slot = slot_of[phase]
        inbox[c, phase, slot] = value
        started = []
        for step in range(1, RING):
            copy = pltpu.make_async_remote_copy(
                src_ref=inbox.at[c, phase, slot],
                dst_ref=inbox.at[c, phase, slot],
                send_sem=red_send.at[c, phase, step],
                recv_sem=red_recv.at[c, phase, step],
                device_id=peer(phase, step),
                device_id_type=MESH,
            )
            copy.start()
            started.append(copy)
        copies.extend(started)
        return started

    def reduce_end(c, phase, started):
        for copy in started:
            copy.wait_recv()
        return jnp.sum(inbox[c, phase], axis=0)

    def message(c):
        value = jnp.where(live, conv_out[c], 0.0)
        sums = jnp.sum(value, axis=0, keepdims=True)
        squares = jnp.sum(value * value, axis=0, keepdims=True)
        row = lax.broadcasted_iota(jnp.int32, (4, chans), 0)
        counted = jnp.where(row == 2, count.astype(F32), 0.0)
        return jnp.where(row == 0, sums, jnp.where(row == 1, squares, counted))

    def moments(total):
        voxels = total[2:3]
        mean = total[0:1] / voxels
        variance = total[1:2] / voxels - mean * mean
        return mean, variance

    pl.semaphore_wait(barrier, 8 + 3 * (RING - 1))
    first_halo = start_exchange(0, features)
    for copy in first_halo:
        copy.start()
    loads[0].wait()
    transpose_weights(0)
    for copy in first_halo:
        copy.wait_recv()
    convolve(0, features, received(0, 0.0))

    started = reduce_start(0, 0, message(0))
    raw = jnp.where(live, conv_out[0], DEAD)
    second_halo = start_exchange(1, raw)
    for copy in second_halo:
        copy.start()
    loads[1].wait()
    transpose_weights(1)
    total = reduce_end(0, 0, started)
    started = reduce_start(0, 1, total)
    total = reduce_end(0, 1, started)
    started = reduce_start(0, 2, total)
    total = reduce_end(0, 2, started)
    mean, variance = moments(total)
    scale = lax.rsqrt(variance + EPSILON) * gain_one[...]

    def activate(x):
        return jnp.maximum((x - mean) * scale + shift_one[...], 0.0)

    for copy in second_halo:
        copy.wait_recv()
    hidden = jnp.where(live, activate(conv_out[0]), 0.0)
    convolve(1, hidden, activate(received(1, DEAD)))

    total = message(1)
    for phase in range(3):
        started = reduce_start(1, phase, total)
        total = reduce_end(1, phase, started)
    mean, variance = moments(total)
    scale = lax.rsqrt(variance + EPSILON) * gain_two[...]
    summed = (conv_out[1] - mean) * scale + shift_two[...] + feat[0, 0].astype(F32)
    out[0, 0] = jnp.where(live, jnp.maximum(summed, 0.0), 0.0).astype(BF16)

    for copy in first_halo + second_halo + copies:
        copy.wait_send()


def solution(mesh):
    n_slab, n_tile = mesh.shape["slab"], mesh.shape["tile"]

    def per_device(
        features,
        counts,
        rulebook,
        face_rows,
        conv_one,
        gain_one,
        shift_one,
        conv_two,
        gain_two,
        shift_two,
    ):
        rows, chans = features.shape[2], features.shape[3]
        vmem = pl.BlockSpec(memory_space=pltpu.VMEM)
        hbm = pl.BlockSpec(memory_space=pl.ANY)
        smem = pl.BlockSpec(memory_space=pltpu.SMEM)
        line = (1, chans)
        return pl.pallas_call(
            functools.partial(kernel, n_slab, n_tile),
            out_shape=jax.ShapeDtypeStruct(features.shape, features.dtype),
            in_specs=[vmem, smem, vmem, vmem, hbm, vmem, vmem, hbm, vmem, vmem],
            out_specs=vmem,
            scratch_shapes=[
                pltpu.VMEM((2, TAPS, chans, chans), BF16),
                pltpu.VMEM((2, chans, TAPS * chans), BF16),
                pltpu.VMEM((rows, 256), BF16),
                pltpu.VMEM((2, 3 * chans, HALF), BF16),
                pltpu.VMEM((TAPS * chans, rows), BF16),
                pltpu.VMEM((2, rows, chans), F32),
                pltpu.VMEM((2, 256, chans), F32),
                pltpu.VMEM((2, HALO, chans), F32),
                pltpu.VMEM((2, 3, RING, 4, chans), F32),
                pltpu.SemaphoreType.DMA((2,)),
                pltpu.SemaphoreType.DMA((2, 8)),
                pltpu.SemaphoreType.DMA((2, 8)),
                pltpu.SemaphoreType.DMA((2, 3, RING)),
                pltpu.SemaphoreType.DMA((2, 3, RING)),
            ],
            compiler_params=pltpu.CompilerParams(
                collective_id=0,
                has_side_effects=True,
                vmem_limit_bytes=60 * 1024 * 1024,
            ),
        )(
            features,
            counts,
            rulebook,
            face_rows,
            conv_one,
            gain_one.reshape(line),
            shift_one.reshape(line),
            conv_two,
            gain_two.reshape(line),
            shift_two.reshape(line),
        )

    grid = P("slab", "tile", None, None)
    return jax.shard_map(
        per_device,
        mesh=mesh,
        in_specs=(grid, P("slab", "tile"), grid, grid, P(), P(), P(), P(), P(), P()),
        out_specs=grid,
        check_vma=False,
    )
```

time: 233 us -> 67.8 us (0.29); the launches traced: 228 us -> 67.6 us
  blocking collectives: 90.3 us -> 0 us
  local copies, waits for them, and re-layouts: 74.2 us -> 3.02 us
  Pallas kernels: 0 us -> 63.9 us
  starting transfers between devices: 27.1 us -> 0 us
  other arithmetic: 24.9 us -> 0 us
  waiting for transfers between devices: 8.04 us -> 0 us
  matrix products: 2.55 us -> 0 us
    psum x8 -> x0, blocking collectives: 90.3 us -> none  [by_axis(): shard = lax.psum(shard, axis)]
    gather x6 -> x0, local copies, waits for them, and re-layouts: 72.4 us -> none  [the longest x4 69.9 us: pick_rows(): gathered = jnp.take(lookup, tap_index.T, axis=0)]
    pallas_call x0 -> x1, Pallas kernels: none -> 63.9 us  [per_device(): pl.pallas_call(functools.partial(kernel, n_slab, n_tile), out_shape=jax.S...]
    ppermute x8 -> x0, starting transfers between devices: 27.1 us -> none  [the longest x4 19.2 us: extended(): lax.ppermute(lax.slice_in_dim(block, block.shape[dim] - width, None, axis...]
    select_n x4 -> x0, other arithmetic: 21.8 us -> none  [the longest x3 21 us: pick_rows(): gathered = jnp.take(lookup, tap_index.T, axis=0)]
    ppermute x8 -> x0, waiting for transfers between devices: 8.04 us -> none  [the longest x4 8.03 us: extended(): lax.ppermute(lax.slice_in_dim(block, 0, width, axis=dim), axis, backward)]
    dot_general x2 -> x0, matrix products: 2.55 us -> none  [pick_rows(): return jnp.dot(gathered, flat_weight, preferred_element_type=jnp.float32)]
  transfers between devices with their start and end apart: 8 -> 0, of which waited for: 3 -> 0; matrix products, arithmetic and copies ran while one was open for 1% -> 0% of each run, Pallas kernels for 0% -> 0%
where the time goes in v1:
time: 67.8 us; the launch traced here: 67.6 us
  Pallas kernels  63.9 us (94%)
  local copies, waits for them, and re-layouts  3.02 us (4%)
    pallas_call x1, Pallas kernels, per_device(): pl.pallas_call(functools.partial(kernel, n_slab, n_tile), out_shape=jax.S...  63.9 us
    unnamed x2, local copies, waits for them, and re-layouts  3.02 us

profile of v1, /device:TPU:1, one launch (start us, length us, event | category | flops | bytes accessed | tf_op | source)
XLA Modules:
  0.0 67.6 jit_solution(9901271775525082952)
XLA Ops:
  0.7 1.4 %copy.11.rb = s32[1,1,27,512]{3,2,1,0:T(8,128)} copy(s32[1,1,27,512]{3,1,2,0:T(1,128)} %param.12) | data formatting | bytes 110592 | tf_op args[2]
  2.1 63.9 %shard_map.100 = bf16[1,1,512,128]{3,2,1,0:T(8,128)(2,1)} custom-call(bf16[1,1,512,128]{3,2,1,0:T(8,128)(2,1)} %feat.1, s32[1,1]{1,0:T(1,128)S(6)} %copy.13.counts, s32[1,1,27,512]{3,2,1,0:T(8,128)} %copy.11.rb, s32[1,1,4,64]{3,2,1,0:T(4,128)} %face.1, bf16[27,128,128]{2,1,0:T(8,128)(2,1)} %w_one.1, f32[1,128]{1,0:T(1,128)} %bitcast.4, f32[1,128]{1,0:T(1,128)} %bitcast.5, ...), custom_call_target="tpu_custom_call" | custom-call | tf_op jit(solution)/shard_map/pallas_call | solution.py:310
  66.0 1.6 %copy.14 = bf16[1,1,512,128]{3,2,1,0:T(8,128)(2,1)} copy(bf16[1,1,512,128]{3,2,1,0:T(8,128)(2,1)} %shard_map.100) | data formatting | bytes 262144
